TPU v7x, 32 devices: a 4x2x2 block of a 4x4x8 slice. The times are simulated.
32 devices in a mesh: dp: 4 (over y, z), ep: 8 (over x, core).
Axes of the slice: x: 4, y: 2, z: 2, core: 2. Of those that a mesh axis runs over, the one named last changes fastest.
The devices are a block of a 4x4x8 slice.
Arguments:
- tokens: bfloat16 [8192, 1024], P(('dp', 'ep')), parts along dimension 0
- expert_ids: int32 [8192, 8], P(('dp', 'ep')), parts along dimension 0
- gate_vals: float32 [8192, 8], P(('dp', 'ep')), parts along dimension 0
- w_gate: bfloat16 [32, 1024, 512], P('ep')
- w_up: bfloat16 [32, 1024, 512], P('ep')
- w_down: bfloat16 [32, 512, 1024], P('ep')
Outputs:
- output: bfloat16 [8192, 1024], P(('dp', 'ep')), parts along dimension 0
There are 4 independent parts. A program takes and returns all parts, laid end to end along the dimension named above; an argument that names none is the same for every part.
All inputs are finite; a program needn't handle non-finite values.
Results may differ from a plain program's by a relative error of at most 0.00631461.
Values are sent between devices in bfloat16 or wider.
A program may use at most 768 MiB of HBM per device.

v0:
```python
import jax
import jax.numpy as jnp
from jax import lax
from jax.sharding import PartitionSpec as P, NamedSharding


def expert_ffn(expert_in, w_gate, w_up, w_down):
    gate_act = jnp.einsum('lcd,ldf->lcf', expert_in, w_gate, preferred_element_type=jnp.float32)
    up_act = jnp.einsum('lcd,ldf->lcf', expert_in, w_up, preferred_element_type=jnp.float32)
    hidden = (jax.nn.silu(gate_act) * up_act).astype(jnp.bfloat16)
    return jnp.einsum('lcf,lfd->lcd', hidden, w_down, preferred_element_type=jnp.float32).astype(jnp.bfloat16)


def serve_rows(recv_rows, recv_gate, w_gate, w_up, w_down, expert_cap):
    member = recv_gate != 0.0
    exp_slot = jnp.cumsum(member.astype(jnp.int32), axis=0) - 1
    fan_mat = (member.T[:, None, :] & (exp_slot.T[:, None, :] == jnp.arange(expert_cap)[None, :, None])).astype(jnp.bfloat16)
    expert_in = jnp.einsum('lcr,rd->lcd', fan_mat, recv_rows, preferred_element_type=jnp.float32).astype(jnp.bfloat16)
    expert_out = expert_ffn(expert_in, w_gate, w_up, w_down)
    row_outs = jnp.einsum('lcr,lcd->lrd', fan_mat, expert_out, preferred_element_type=jnp.float32)
    dev_sum = jnp.sum(recv_gate.T[:, :, None] * row_outs, axis=0)
    return dev_sum.astype(jnp.bfloat16)


def send_tables(expert_ids, gate_vals, groups, local_count, pair_cap):
    tok_dev = expert_ids.shape[0]
    chosen = jnp.any((expert_ids // local_count)[:, :, None] == jnp.arange(groups)[None, None, :], axis=1)
    send_rank = jnp.cumsum(chosen.astype(jnp.int32), axis=0) - 1
    pack_mask = chosen.T[:, None, :] & (send_rank.T[:, None, :] == jnp.arange(pair_cap)[None, :, None])
    gate_dense = jnp.sum(jnp.where(expert_ids[:, :, None] == jnp.arange(groups * local_count)[None, None, :], gate_vals[:, :, None], 0.0), axis=1)
    gate_t = jnp.swapaxes(gate_dense.reshape(tok_dev, groups, local_count), 0, 1)
    send_gate = jnp.sum(jnp.where(pack_mask[:, :, :, None], gate_t[:, None, :, :], 0.0), axis=2)
    return pack_mask.astype(jnp.bfloat16), send_gate


def solution(mesh):
    groups = mesh.shape['ep']
    row_spec = P(('dp', 'ep'))
    expert_spec = P('ep')

    def device_step(tokens, expert_ids, gate_vals, w_gate, w_up, w_down):
        tok_dev, top_k = expert_ids.shape
        d_model = tokens.shape[1]
        local_count = w_gate.shape[0]
        pair_cap = tok_dev * (top_k // 2) // groups
        expert_cap = tok_dev * top_k // local_count
        row_count = groups * pair_cap
        pack_mat, send_gate = send_tables(expert_ids, gate_vals, groups, local_count, pair_cap)
        send_rows = jnp.einsum('qct,td->qcd', pack_mat, tokens, preferred_element_type=jnp.float32).astype(jnp.bfloat16)
        recv_rows = lax.all_to_all(send_rows, 'ep', 0, 0, tiled=True)
        recv_gate = lax.all_to_all(send_gate, 'ep', 0, 0, tiled=True)
        dev_sum = serve_rows(recv_rows.reshape(row_count, d_model), recv_gate.reshape(row_count, local_count), w_gate, w_up, w_down, expert_cap)
        returned = lax.all_to_all(dev_sum.reshape(groups, pair_cap, d_model), 'ep', 0, 0, tiled=True)
        moe_sum = jnp.einsum('qct,qcd->td', pack_mat, returned, preferred_element_type=jnp.float32)
        return (tokens.astype(jnp.float32) + moe_sum).astype(jnp.bfloat16)

    return jax.shard_map(device_step, mesh=mesh, in_specs=(row_spec, row_spec, row_spec, expert_spec, expert_spec, expert_spec), out_specs=row_spec, check_vma=False)
```

profile of v0, /device:TPU:81, one launch (start us, length us, event | category | flops | bytes accessed | tf_op | source)
XLA Modules:
  0.0 109.2 jit_solution(12067623368970093065)
XLA Ops:
  0.0 0.7 add_select_fusion
  0.7 0.6 reduce-window.14
  1.3 0.2 slice_reduce_fusion.1
  1.6 0.1 add_bitcast_fusion.1
  1.7 0.8 select_reduce_fusion.1
  2.4 0.7 fusion.15
  3.2 0.5 copy.27
  3.6 1.3 %select_reduce_fusion = f32[8,128,4]{1,2,0:T(4,128)} fusion(f32[8,256,4]{1,2,0:T(4,128)S(1)} %bitcast.53, pred[8,128,256]{2,1,0:T(8,128)(4,1)S(1)} %copy.27), kind=kLoop, calls=%fused_computation.8 | loop fusion | flops 2093056 | bytes 311296 | tf_op jit(solution)/shard_map/reduce_sum | solution.py:32
  4.9 6.0 %all-to-all-start = ((f32[8,128,4]{1,2,0:T(4,128)}), f32[8,128,4]{1,2,0:T(4,128)S(1)}, u32[]{:S(2)}, u32[]{:S(2)}) async-start(f32[8,128,4]{1,2,0:T(4,128)} %select_reduce_fusion), calls=%async_computation | async-start | bytes 32768 | tf_op jit(solution)/shard_map/all_to_all | solution.py:51
  10.9 3.8 %convolution_convert_fusion = bf16[8,128,1024]{2,1,0:T(8,128)(2,1)} fusion(bf16[256,1024]{1,0:T(8,128)(2,1)} %param.6, s32[8,256]{1,0:T(8,128)S(1)} %add_bitcast_fusion.1, pred[8,256]{1,0:T(8,128)(4,1)S(1)} %bitcast.57), kind=kOutput, calls=%fused_computation.12 | convolution fusion | flops 538443776 | bytes 2631680 | tf_op jit(solution)/shard_map/qct,td->qcd/dot_general | solution.py:49
  14.7 0.7 all-to-all-done
  15.3 4.2 %all-to-all-start.1 = ((bf16[8,128,1024]{2,1,0:T(8,128)(2,1)}), bf16[8,128,1024]{2,1,0:T(8,128)(2,1)S(1)}, u32[]{:S(2)}, u32[]{:S(2)}) async-start(bf16[8,128,1024]{2,1,0:T(8,128)(2,1)} %convolution_convert_fusion), calls=%async_computation.1 | async-start | bytes 4194304 | tf_op jit(solution)/shard_map/all_to_all | solution.py:50
  19.6 1.1 %reduce-window.16 = s32[4,8,128]{2,1,0:T(8,128)S(1)} reduce-window(s32[4,8,128]{2,1,0:T(8,128)S(1)} %bitcast.55, s32[]{:T(128)} %constant.27.clone.1), window={size=1x1x128 pad=0_0x0_0x127_0}, to_apply=%region_5.6 | reduce-window | flops 520192 | bytes 32772 | tf_op jit(solution)/shard_map/reduce-window.2
  20.7 0.2 slice_reduce_fusion
  21.0 0.2 reduce-window.19
  21.1 0.1 add_bitcast_fusion
  21.2 24.4 %all-to-all-done.1 = bf16[8,128,1024]{2,1,0:T(8,128)(2,1)S(1)} async-done(((bf16[8,128,1024]{2,1,0:T(8,128)(2,1)}), bf16[8,128,1024]{2,1,0:T(8,128)(2,1)S(1)}, u32[]{:S(2)}, u32[]{:S(2)}) %all-to-all-start.1) | async-done | bytes 2097184 | tf_op jit(solution)/shard_map/all_to_all | solution.py:50
  45.7 0.0 copy-start.1
  45.7 5.7 %fusion.9 = bf16[4,512,1024]{2,1,0:T(8,128)(2,1)S(1)} fusion(bf16[1024,1024,1]{1,0,2:T(8,128)(2,1)S(1)} %bitcast.51, s32[4,1024]{1,0:T(4,128)S(1)} %bitcast.59, pred[4,1024]{1,0:T(4,128)(4,1)S(1)} %get-tuple-element.6), kind=kOutput, calls=%fused_computation.11 | convolution fusion | flops 4301258752 | bytes 6311936 | tf_op jit(solution)/shard_map/lcr,rd->lcd/dot_general | solution.py:18
  51.3 0.0 copy-start.2
  51.4 2.0 %copy-done.2 = bf16[4,512,1024]{2,1,0:T(8,128)(2,1)} copy-done((bf16[4,512,1024]{2,1,0:T(8,128)(2,1)}, bf16[4,512,1024]{2,1,0:T(8,128)(2,1)S(1)}, u32[]{:S(2)}) %copy-start.2) | copy-done | bytes 4194328
  53.3 0.0 copy-done.1
  53.3 4.3 %fusion.25 = f32[4,512,512]{2,1,0:T(8,128)} fusion(bf16[4,512,1024]{2,1,0:T(8,128)(2,1)S(1)} %fusion.9, bf16[4,1024,512]{2,1,0:T(8,128)(2,1)S(1)} %copy-done.1), kind=kOutput, calls=%fused_computation.42 | convolution fusion | flops 2147483648 | bytes 12582912 | tf_op jit(solution)/shard_map/lcd,ldf->lcf/dot_general | solution.py:8
  57.6 12.5 %fusion.12 = bf16[4,512,1024]{2,1,0:T(8,128)(2,1)} fusion(bf16[4,512,1024]{2,1,0:T(8,128)(2,1)} %param.11, f32[4,512,512]{2,1,0:T(8,128)} %fusion.25, bf16[4,512,1024]{2,1,0:T(8,128)(2,1)} %copy-done.2, bf16[4,1024,512]{2,1,0:T(8,128)(2,1)} %param.10), kind=kOutput, calls=%fused_computation.13 | convolution fusion | flops 4301258752 | bytes 20971520 | tf_op jit(solution)/shard_map/lcf,lfd->lcd/dot_general | solution.py:11
  70.1 7.1 %multiply_reduce_fusion = bf16[1024,1024]{1,0:T(8,128)(2,1)S(1)} fusion(f32[4,1024]{1,0:T(4,128)S(1)} %bitcast.54, bf16[4,512,1024]{2,1,0:T(8,128)(2,1)} %fusion.12, s32[4,1024]{1,0:T(4,128)S(1)} %bitcast.60, pred[4,1024]{1,0:T(4,128)(4,1)S(1)} %get-tuple-element.6), kind=kOutput, calls=%fused_computation | convolution fusion | flops 4306501632 | bytes 6328320 | tf_op jit(solution)/shard_map/lcr,lcd->lrd/dot_general | solution.py:20
  77.2 0.0 copy-start
  77.2 30.0 %all_to_all.15 = bf16[8,128,1024]{2,1,0:T(8,128)(2,1)S(1)} all-to-all(bf16[8,128,1024]{2,1,0:T(8,128)(2,1)S(1)} %bitcast.52), channel_id=1, replica_groups=mesh['dp'=4,'ep'=8] {'ep'}, dimensions={0} | all-to-all | bytes 4194304 | tf_op jit(solution)/shard_map/all_to_all | solution.py:53
  107.2 0.0 copy-done
  107.2 2.0 %fusion.14 = bf16[256,1024]{1,0:T(8,128)(2,1)} fusion(bf16[8,128,1024]{2,1,0:T(8,128)(2,1)S(1)} %all_to_all.15, bf16[256,1024]{1,0:T(8,128)(2,1)S(1)} %copy-done, s32[8,256]{1,0:T(8,128)S(1)} %add_bitcast_fusion.1, pred[8,256]{1,0:T(8,128)(4,1)S(1)} %bitcast.58), kind=kOutput, calls=%fused_computation.16 | convolution fusion | flops 538181632 | bytes 3155968 | tf_op jit(solution)/shard_map/qct,qcd->td/dot_general | solution.py:54
  (8 shorter events, 0.1 us)
Async XLA Ops:
  4.9 10.5 %all-to-all-start = ((f32[8,128,4]{1,2,0:T(4,128)}), f32[8,128,4]{1,2,0:T(4,128)S(1)}, u32[]{:S(2)}, u32[]{:S(2)}) async-start(f32[8,128,4]{1,2,0:T(4,128)} %select_reduce_fusion), calls=%async_computation | async-start | bytes 32768 | tf_op jit(solution)/shard_map/all_to_all | solution.py:51
  15.3 30.3 %all-to-all-start.1 = ((bf16[8,128,1024]{2,1,0:T(8,128)(2,1)}), bf16[8,128,1024]{2,1,0:T(8,128)(2,1)S(1)}, u32[]{:S(2)}, u32[]{:S(2)}) async-start(bf16[8,128,1024]{2,1,0:T(8,128)(2,1)} %convolution_convert_fusion), calls=%async_computation.1 | async-start | bytes 4194304 | tf_op jit(solution)/shard_map/all_to_all | solution.py:50
  45.7 7.6 %copy-start.1 = (bf16[4,1024,512]{2,1,0:T(8,128)(2,1)S(1)}, bf16[4,1024,512]{2,1,0:T(8,128)(2,1)}, u32[]{:S(2)}) copy-start(bf16[4,1024,512]{2,1,0:T(8,128)(2,1)} %param.9) | copy-start | bytes 12582916
  51.3 2.0 %copy-start.2 = (bf16[4,512,1024]{2,1,0:T(8,128)(2,1)}, bf16[4,512,1024]{2,1,0:T(8,128)(2,1)S(1)}, u32[]{:S(2)}) copy-start(bf16[4,512,1024]{2,1,0:T(8,128)(2,1)S(1)} %fusion.9) | copy-start | bytes 12582916
  77.2 30.0 %copy-start = (bf16[256,1024]{1,0:T(8,128)(2,1)S(1)}, bf16[256,1024]{1,0:T(8,128)(2,1)}, u32[]{:S(2)}) copy-start(bf16[256,1024]{1,0:T(8,128)(2,1)} %param.6) | copy-start | bytes 1572868
where the time goes:
time: 110 us; the launch traced here: 109 us
  matrix products  35.3 us (32%)
  blocking collectives  30 us (27%)
  waiting for transfers between devices  25.1 us (23%)
  starting transfers between devices  10.2 us (9%)
  other arithmetic  5.59 us (5%)
  local copies, waits for them, and re-layouts  2.88 us (3%)
    all_to_all x1, blocking collectives, device_step(): lax.all_to_all(dev_sum.reshape(groups, pair_cap, d_model), 'ep', 0, 0, ti...  30 us
    all_to_all x1, waiting for transfers between devices, device_step(): recv_rows = lax.all_to_all(send_rows, 'ep', 0, 0, tiled=True)  24.4 us
    dot_general x1, matrix products, expert_ffn(): jnp.einsum('lcf,lfd->lcd', hidden, w_down, preferred_element_type=jnp.flo...  12.5 us
    dot_general x1, matrix products, serve_rows(): jnp.einsum('lcr,lcd->lrd', fan_mat, expert_out, preferred_element_type=jn...  7.14 us
    all_to_all x1, starting transfers between devices, device_step(): recv_gate = lax.all_to_all(send_gate, 'ep', 0, 0, tiled=True)  6.01 us
    dot_general x1, matrix products, serve_rows(): jnp.einsum('lcr,rd->lcd', fan_mat, recv_rows, preferred_element_type=jnp....  5.66 us
    dot_general x1, matrix products, expert_ffn(): jnp.einsum('lcd,ldf->lcf', expert_in, w_gate, preferred_element_type=jnp....  4.26 us
    all_to_all x1, starting transfers between devices, device_step(): recv_rows = lax.all_to_all(send_rows, 'ep', 0, 0, tiled=True)  4.23 us
  transfers between devices with their start and end apart: 2, of which 2 were waited for; matrix products, arithmetic and copies ran while one was open for 5% of the time, Pallas kernels for 0%

commit v1 on v0

v1 whole, which is shorter than its diff:
```python
import functools

import jax
import jax.numpy as jnp
from jax import lax
from jax.experimental import pallas as pl
from jax.experimental.pallas import tpu as pltpu
from jax.sharding import PartitionSpec as P

MESH = pl.DeviceIdType.MESH
F32, BF16 = jnp.float32, jnp.bfloat16
OWN, MATE, R0, R1, O0, O1, L0, L1 = range(8)


def back(slot):
    return (-(slot // 2)) % 4 * 2 + slot % 2


def kernel(tok, ids, gates, wg_hbm, wu_hbm, wd_hbm, out,
           xs, tables, mytab, tri, wg, wu, wd, sums, home, acc, rank_home,
           tok_sem, w_sem, xs_send, xs_recv, tab_send, tab_recv, s_send, s_recv):
    rows, half = tok.shape[0], tok.shape[0] // 2
    n_exp = wg.shape[0]
    me = lax.axis_index("ep")
    x = me // 2
    c = me - 2 * x
    x_of = [lax.rem(x + d, 4) for d in range(4)]
    dev = [2 * x_of[s // 2] + (1 - c if s % 2 else c) for s in range(8)]

    def remote(src, dst, send, recv, slot):
        return pltpu.make_async_remote_copy(src_ref=src, dst_ref=dst, send_sem=send, recv_sem=recv,
                                            device_id={"ep": dev[slot]}, device_id_type=MESH)

    tok_in = pltpu.make_async_copy(tok, xs.at[OWN], tok_sem)
    tok_in.start()
    weights = [[pltpu.make_async_copy(h.at[e], v.at[e], w_sem.at[i, e]) for i, (h, v) in
                enumerate(((wg_hbm, wg), (wu_hbm, wu), (wd_hbm, wd)))] for e in range(n_exp)]
    for e in range(n_exp):
        for cp in weights[e]:
            cp.start()

    barrier = pltpu.get_barrier_semaphore()
    for s in range(1, 8):
        pl.semaphore_signal(barrier, inc=1, device_id={"ep": dev[s]}, device_id_type=MESH)
    pl.semaphore_wait(barrier, 7)
    tok_in.wait()

    halves = (pl.ds(0, half), pl.ds(half, half))

    def block(slot_src, h, to, sem):
        owner = (slot_src // 2 - to // 2) % 4 * 2 + (slot_src % 2 + to % 2) % 2
        return remote(xs.at[slot_src, halves[h]], xs.at[owner, halves[h]], xs_send.at[sem], xs_recv.at[owner, h], to)

    sends = []

    def go(cp):
        cp.start()
        sends.append(cp)

    def arrived(slot, h):
        pltpu.make_async_remote_copy(src_ref=xs.at[slot, halves[h]], dst_ref=xs.at[slot, halves[h]], send_sem=xs_send.at[0],
                                     recv_sem=xs_recv.at[slot, h], device_id={"ep": dev[MATE]},
                                     device_id_type=MESH).wait_recv()

    go(block(OWN, 0, R0, 0))
    go(block(OWN, 1, L0, 1))
    go(block(OWN, 1, R0, 2))
    go(block(OWN, 0, L0, 3))
    go(block(OWN, 0, MATE, 4))
    go(block(OWN, 1, MATE, 5))

    row8 = lax.broadcasted_iota(jnp.int32, (2 * n_exp, half), 0)
    in_first = row8 < n_exp
    exp_of = jnp.where(in_first, row8, row8 - n_exp)
    id_rep = [jnp.where(in_first, ids[j:j + 1, 0:half], ids[j:j + 1, half:rows]) for j in range(ids.shape[0])]
    g_rep = [jnp.where(in_first, gates[j:j + 1, 0:half], gates[j:j + 1, half:rows]) for j in range(ids.shape[0])]
    for s in range(8):
        want = exp_of + dev[s] * n_exp
        tab = jnp.zeros((2 * n_exp, half), F32)
        for j in range(ids.shape[0]):
            tab = tab + jnp.where(id_rep[j] == want, g_rep[j], 0.0)
        mytab[s] = tab
    for i, s in enumerate((MATE, R0, L0, R1, L1, O0, O1)):
        go(remote(mytab.at[s], tables.at[back(s)], tab_send.at[i], tab_recv.at[back(s)], s))

    def table_arrived(slot):
        pltpu.make_async_remote_copy(src_ref=tables.at[slot], dst_ref=tables.at[slot], send_sem=tab_send.at[0],
                                     recv_sem=tab_recv.at[slot], device_id={"ep": dev[MATE]},
                                     device_id_type=MESH).wait_recv()

    tri[...] = (lax.broadcasted_iota(jnp.int32, (rows, rows), 0) <=
                lax.broadcasted_iota(jnp.int32, (rows, rows), 1)).astype(F32).astype(BF16)

    def place(tab):
        hit = (tab != 0.0).astype(F32)
        one = [jnp.max(hit[i * n_exp:(i + 1) * n_exp], axis=0, keepdims=True) for i in range(2)]
        hit = jnp.concatenate(one, axis=1)
        count = jnp.dot(jnp.broadcast_to(hit, (16, rows)).astype(BF16), tri[...], preferred_element_type=F32)[0:1]
        return jnp.where(hit > 0.0, count - 1.0, -1.0)

    def one_hot(where):
        slot_row = lax.broadcasted_iota(jnp.int32, (half, rows), 0).astype(F32)
        return (slot_row == where).astype(F32)

    for s in range(8):
        rank_home[s:s + 1] = place(mytab[s])

    def serve(slot, first=False):
        tab = mytab[OWN] if slot == OWN else tables[slot]
        pick = one_hot(place(tab))
        row_in = jnp.dot(pick.astype(BF16), xs[slot], preferred_element_type=F32).astype(BF16)
        part = [lax.dot_general(pick[:, i * half:(i + 1) * half], tab, (((1,), (1,)), ((), ())),
                                precision=lax.Precision.HIGHEST, preferred_element_type=F32) for i in range(2)]
        total = jnp.zeros((half, xs.shape[2]), F32)
        for e in range(n_exp):
            if first:
                for cp in weights[e]:
                    cp.wait()
            a = jnp.dot(row_in, wg[e], preferred_element_type=F32)
            b = jnp.dot(row_in, wu[e], preferred_element_type=F32)
            hid = (a * (1.0 / (1.0 + jnp.exp(-a))) * b).astype(BF16)
            y = jnp.dot(hid, wd[e], preferred_element_type=F32).astype(BF16).astype(F32)
            g = part[0][:, e:e + 1] + part[1][:, n_exp + e:n_exp + e + 1]
            total = total + jnp.where(g != 0.0, g * y, 0.0)
        return total.astype(BF16)

    def answer(slot):
        sums[slot] = serve(slot)
        go(remote(sums.at[slot], home.at[back(slot)], s_send.at[slot], s_recv.at[back(slot)], slot))

    home[OWN] = serve(OWN, first=True)
    for h in range(2):
        arrived(MATE, h)
    table_arrived(MATE)
    answer(MATE)
    arrived(L0, 0)
    go(block(L0, 0, R0, 6))
    go(block(L0, 0, MATE, 8))
    arrived(R0, 1)
    go(block(R0, 1, L0, 7))
    go(block(R0, 1, MATE, 9))
    arrived(L0, 1)
    go(block(L0, 1, MATE, 10))
    arrived(R0, 0)
    go(block(R0, 0, MATE, 11))
    table_arrived(L0)
    answer(L0)
    table_arrived(R0)
    answer(R0)
    for h in range(2):
        arrived(L1, h)
    table_arrived(L1)
    answer(L1)
    for h in range(2):
        arrived(O0, h)
        go(block(O0, h, MATE, 12 + h))
    for h in range(2):
        arrived(R1, h)
    table_arrived(R1)
    answer(R1)
    table_arrived(O0)
    answer(O0)
    for h in range(2):
        arrived(O1, h)
    table_arrived(O1)
    answer(O1)

    def back_home(pair):
        pick = jnp.concatenate([one_hot(rank_home[2 * pair + i:2 * pair + i + 1]) for i in range(2)], axis=0).astype(BF16)
        got = home[pl.ds(2 * pair, 2)].reshape(rows, home.shape[2])
        return lax.dot_general(pick, got, (((0,), (0,)), ((), ())), preferred_element_type=F32)

    def sum_arrived(slot):
        pltpu.make_async_remote_copy(src_ref=home.at[slot], dst_ref=home.at[slot], send_sem=s_send.at[0],
                                     recv_sem=s_recv.at[slot], device_id={"ep": dev[MATE]},
                                     device_id_type=MESH).wait_recv()

    sum_arrived(MATE)
    acc[...] = xs[OWN].astype(F32) + back_home(0)
    for s in (L0, L1):
        sum_arrived(s)
    acc[...] += back_home(3)
    for s in (R0, R1):
        sum_arrived(s)
    acc[...] += back_home(1)
    for s in (O0, O1):
        sum_arrived(s)
    out[...] = (acc[...] + back_home(2)).astype(BF16)
    for cp in sends:
        cp.wait_send()


def solution(mesh):
    row_spec = P(('dp', 'ep'))
    expert_spec = P('ep')
    group = mesh.shape['ep']
    assert group == 8

    def device_step(tokens, expert_ids, gate_vals, w_gate, w_up, w_down):
        rows, width = tokens.shape
        n_exp, _, hidden = w_gate.shape
        half = rows // 2
        any_spec = pl.BlockSpec(memory_space=pl.ANY)
        vmem_spec = pl.BlockSpec(memory_space=pltpu.VMEM)
        dma = pltpu.SemaphoreType.DMA
        return pl.pallas_call(
            kernel,
            out_shape=jax.ShapeDtypeStruct((rows, width), BF16),
            in_specs=[any_spec, vmem_spec, vmem_spec, any_spec, any_spec, any_spec],
            out_specs=vmem_spec,
            scratch_shapes=[
                pltpu.VMEM((group, rows, width), BF16),
                pltpu.VMEM((group, 2 * n_exp, half), F32),
                pltpu.VMEM((group, 2 * n_exp, half), F32),
                pltpu.VMEM((rows, rows), BF16),
                pltpu.VMEM((n_exp, width, hidden), BF16),
                pltpu.VMEM((n_exp, width, hidden), BF16),
                pltpu.VMEM((n_exp, hidden, width), BF16),
                pltpu.VMEM((group, half, width), BF16),
                pltpu.VMEM((group, half, width), BF16),
                pltpu.VMEM((rows, width), F32),
                pltpu.VMEM((group, rows), F32),
                dma, dma((3, n_exp)), dma((14,)), dma((group, 2)), dma((7,)), dma((group,)), dma((group,)), dma((group,)),
            ],
            compiler_params=pltpu.CompilerParams(collective_id=0, has_side_effects=True, vmem_limit_bytes=60 * 1024 * 1024),
        )(tokens, expert_ids.T, gate_vals.T, w_gate, w_up, w_down)

    return jax.shard_map(device_step, mesh=mesh, in_specs=(row_spec, row_spec, row_spec, expert_spec, expert_spec, expert_spec),
                         out_specs=row_spec, check_vma=False)
```

time: 110 us -> 54.6 us (0.50)
  Pallas kernels: 0 us -> 52.5 us
  matrix products: 35.3 us -> 0 us
  blocking collectives: 30 us -> 0 us
  waiting for transfers between devices: 25.1 us -> 0 us
  starting transfers between devices: 10.2 us -> 0 us
  other arithmetic: 5.59 us -> 0 us
    pallas_call x0 -> x1, Pallas kernels: none -> 52.5 us  [device_step(): pl.pallas_call(kernel, out_shape=jax.ShapeDtypeStruct((rows, width), BF16...]
    dot_general x6 -> x0, matrix products: 35.3 us -> none  [the longest x1 12.5 us: expert_ffn(): jnp.einsum('lcf,lfd->lcd', hidden, w_down, preferred_element_type=jnp.flo...]
    all_to_all x1 -> x0, blocking collectives: 30 us -> none  [device_step(): lax.all_to_all(dev_sum.reshape(groups, pair_cap, d_model), 'ep', 0, 0, ti...]
    all_to_all x2 -> x0, waiting for transfers between devices: 25.1 us -> none  [the longest x1 24.4 us: device_step(): recv_rows = lax.all_to_all(send_rows, 'ep', 0, 0, tiled=True)]
    all_to_all x2 -> x0, starting transfers between devices: 10.2 us -> none  [the longest x1 6.01 us: device_step(): recv_gate = lax.all_to_all(send_gate, 'ep', 0, 0, tiled=True)]
    reduce_sum x2 -> x0, other arithmetic: 2.04 us -> none  [the longest x1 1.28 us: send_tables(): jnp.sum(jnp.where(pack_mask[:, :, :, None], gate_t[:, None, :, :], 0.0),...]
    another operation x5 -> x0, other arithmetic: 1.96 us -> none
  transfers between devices with their start and end apart: 2 -> 0, of which waited for: 2 -> 0; matrix products, arithmetic and copies ran while one was open for 5% -> 0% of each run, Pallas kernels for 0% -> 0%
where the time goes in v1:
time: 54.6 us; the launch traced here: 54.4 us
  Pallas kernels  52.5 us (96%)
  local copies, waits for them, and re-layouts  1.87 us (3%)
    pallas_call x1, Pallas kernels, device_step(): pl.pallas_call(kernel, out_shape=jax.ShapeDtypeStruct((rows, width), BF16...  52.5 us
    unnamed x1, local copies, waits for them, and re-layouts  1.87 us

profile of v1, /device:TPU:81, one launch (start us, length us, event | category | flops | bytes accessed | tf_op | source)
XLA Modules:
  0.0 54.4 jit_solution(12173489674079541288)
XLA Ops:
  0.0 52.5 %shard_map.64 = bf16[256,1024]{1,0:T(8,128)(2,1)} custom-call(bf16[256,1024]{1,0:T(8,128)(2,1)} %tok.1, s32[8,256]{1,0:T(8,128)} %bitcast.2, f32[8,256]{1,0:T(8,128)} %bitcast.3, bf16[4,1024,512]{2,1,0:T(8,128)(2,1)} %wg_hbm.1, bf16[4,1024,512]{2,1,0:T(8,128)(2,1)} %wu_hbm.1, bf16[4,512,1024]{2,1,0:T(8,128)(2,1)} %wd_hbm.1), custom_call_target="tpu_custom_call" | custom-call | tf_op jit(solution)/shard_map/pallas_call | solution.py:206
  52.5 1.9 %copy.8 = bf16[256,1024]{1,0:T(8,128)(2,1)} copy(bf16[256,1024]{1,0:T(8,128)(2,1)} %shard_map.64) | data formatting | bytes 1048576

commit v2 on v0

v2 whole, which is shorter than its diff:
```python
import functools

import jax
import jax.numpy as jnp
from jax import lax
from jax.experimental import pallas as pl
from jax.experimental.pallas import tpu as pltpu
from jax.sharding import PartitionSpec as P

MESH = pl.DeviceIdType.MESH
F32, BF16 = jnp.float32, jnp.bfloat16
OWN, MATE, A0, B0, A1, B1, O0, O1 = range(8)
CHIP = (0, 0, 1, 3, 1, 3, 2, 2)
CORE = (0, 1, 0, 0, 1, 1, 0, 1)


def seen_from(owner, reader):
    want = (CHIP[owner] ^ CHIP[reader], CORE[owner] ^ CORE[reader])
    return [s for s in range(8) if (CHIP[s], CORE[s]) == want][0]


def kernel(tok, ids_hbm, gates_hbm, wg_hbm, wu_hbm, wd_hbm, out,
           xs, tables, mytab, tri, wgu, wd, row_in, sums, home, acc, rank_home, ids, gates,
           tok_sem, route_sem, w_sem, xs_send, tab_send, s_send, xs_recv, half_recv, tab_recv, s_recv):
    rows, half = tok.shape[0], tok.shape[0] // 2
    n_exp = wd.shape[0]
    me = lax.axis_index("ep")
    x = me // 2
    c = me - 2 * x
    x_of = (x, x + 1 - 2 * lax.rem(x, 2), lax.rem(x + 2, 4), 3 - x)
    dev = [2 * x_of[CHIP[s]] + (1 - c if CORE[s] else c) for s in range(8)]

    def remote(src, dst, send, recv, slot):
        return pltpu.make_async_remote_copy(src_ref=src, dst_ref=dst, send_sem=send, recv_sem=recv,
                                            device_id={"ep": dev[slot]}, device_id_type=MESH)

    def wait_for(ref, sem):
        remote(ref, ref, xs_send, sem, MATE).wait_recv()

    tok_in = pltpu.make_async_copy(tok, xs.at[OWN], tok_sem)
    tok_in.start()
    route_in = [pltpu.make_async_copy(h, v, route_sem.at[i]) for i, (h, v) in enumerate(((ids_hbm, ids), (gates_hbm, gates)))]
    for cp in route_in:
        cp.start()
    barrier = pltpu.get_barrier_semaphore()
    for s in range(1, 8):
        pl.semaphore_signal(barrier, inc=1, device_id={"ep": dev[s]}, device_id_type=MESH)
    pl.semaphore_wait(barrier, 7)
    tok_in.wait()

    part = (pl.ds(0, half), pl.ds(half, half))
    whole = pl.ds(0, rows)

    def pass_on(owner, h, to, recv):
        slot = seen_from(owner, to)
        remote(xs.at[owner, h], xs.at[slot, h], xs_send, recv, to).start()

    for i in range(2):
        pass_on(OWN, part[i], A0, half_recv.at[0, i])
        pass_on(OWN, part[1 - i], B0, half_recv.at[1, i])
    pass_on(OWN, whole, MATE, xs_recv.at[MATE])
    w_in = [pltpu.make_async_copy(wg_hbm, wgu.at[0], w_sem.at[0]), pltpu.make_async_copy(wu_hbm, wgu.at[1], w_sem.at[0]),
            pltpu.make_async_copy(wd_hbm, wd, w_sem.at[1])]
    for cp in w_in:
        cp.start()

    for cp in route_in:
        cp.wait()
    row8 = lax.broadcasted_iota(jnp.int32, (2 * n_exp, half), 0)
    in_first = row8 < n_exp
    exp_of = jnp.where(in_first, row8, row8 - n_exp)
    id_rep = [jnp.where(in_first, ids[j:j + 1, 0:half], ids[j:j + 1, half:rows]) for j in range(ids.shape[0])]
    g_rep = [jnp.where(in_first, gates[j:j + 1, 0:half], gates[j:j + 1, half:rows]) for j in range(ids.shape[0])]
    for s in range(8):
        want = exp_of + dev[s] * n_exp
        tab = jnp.zeros((2 * n_exp, half), F32)
        for j in range(ids.shape[0]):
            tab = tab + jnp.where(id_rep[j] == want, g_rep[j], 0.0)
        mytab[s] = tab
    tri[...] = (lax.broadcasted_iota(jnp.int32, (rows, rows), 0) <=
                lax.broadcasted_iota(jnp.int32, (rows, rows), 1)).astype(F32).astype(BF16)
    for s in range(1, 8):
        remote(mytab.at[s], tables.at[s], tab_send, tab_recv.at[s // 2], s).start()

    def place(tab):
        hit = (tab != 0.0).astype(F32)
        one = [jnp.max(hit[i * n_exp:(i + 1) * n_exp], axis=0, keepdims=True) for i in range(2)]
        hit = jnp.concatenate(one, axis=1)
        count = jnp.dot(jnp.broadcast_to(hit, (16, rows)).astype(BF16), tri[...], preferred_element_type=F32)[0:1]
        return jnp.where(hit > 0.0, count - 1.0, -1.0)

    def one_hot(where):
        slot_row = lax.broadcasted_iota(jnp.int32, (half, rows), 0).astype(F32)
        return (slot_row == where).astype(F32)

    for s in range(8):
        rank_home[s:s + 1] = place(mytab[s])

    def serve(pair):
        weight = []
        for i, slot in enumerate(pair):
            tab = mytab[OWN] if slot == OWN else tables[slot]
            pick = one_hot(rank_home[OWN:OWN + 1] if slot == OWN else place(tab))
            row_in[part[i], :] = jnp.dot(pick.astype(BF16), xs[slot], preferred_element_type=F32).astype(BF16)
            g = [lax.dot_general(pick[:, j * half:(j + 1) * half], tab, (((1,), (1,)), ((), ())),
                                 precision=lax.Precision.HIGHEST, preferred_element_type=F32) for j in range(2)]
            weight.append([g[0][:, e:e + 1] + g[1][:, n_exp + e:n_exp + e + 1] for e in range(n_exp)])
        total = jnp.zeros(acc.shape, F32)
        for e in range(n_exp):
            a = jnp.dot(row_in[...], wgu[0, e], preferred_element_type=F32)
            b = jnp.dot(row_in[...], wgu[1, e], preferred_element_type=F32)
            hid = (a * (1.0 / (1.0 + jnp.exp(-a))) * b).astype(BF16)
            y = jnp.dot(hid, wd[e], preferred_element_type=F32).astype(BF16).astype(F32)
            g = jnp.concatenate([w[e] for w in weight], axis=0)
            total = total + jnp.where(g != 0.0, g * y, 0.0)
        total = total.astype(BF16)
        for i, slot in enumerate(pair):
            (home if slot == OWN else sums)[slot] = total[i * half:(i + 1) * half]
        for slot in pair:
            if slot != OWN:
                remote(sums.at[slot], home.at[slot], s_send, s_recv.at[slot // 2], slot).start()

    def tables_of(pair):
        wait_for(tables.at[pl.ds(pair[0], 2)] if pair[0] else tables.at[MATE], tab_recv.at[pair[0] // 2])

    wait_for(xs.at[MATE], xs_recv.at[MATE])
    tables_of((OWN, MATE))
    wait_for(wgu, w_sem.at[0])
    w_in[2].wait()
    serve((OWN, MATE))
    for slot, on, i in ((A0, B0, 0), (B0, A0, 1)):
        wait_for(xs.at[slot, part[i]], half_recv.at[i, 0])
        pass_on(slot, part[i], on, xs_recv.at[O0])
        pass_on(slot, part[i], MATE, xs_recv.at[seen_from(slot, MATE)])
    for slot, i in ((A0, 0), (B0, 1)):
        wait_for(xs.at[slot, part[1 - i]], half_recv.at[i, 1])
        pass_on(slot, part[1 - i], MATE, xs_recv.at[seen_from(slot, MATE)])
    tables_of((A0, B0))
    serve((A0, B0))
    wait_for(xs.at[A1], xs_recv.at[A1])
    wait_for(xs.at[B1], xs_recv.at[B1])
    tables_of((A1, B1))
    serve((A1, B1))
    wait_for(xs.at[O0], xs_recv.at[O0])
    pass_on(O0, whole, MATE, xs_recv.at[O1])
    wait_for(xs.at[O1], xs_recv.at[O1])
    tables_of((O0, O1))
    serve((O0, O1))

    def back_home(pair):
        pick = jnp.concatenate([one_hot(rank_home[s:s + 1]) for s in (pair, pair + 1)], axis=0).astype(BF16)
        got = home[pl.ds(pair, 2)].reshape(rows, home.shape[2])
        return lax.dot_general(pick, got, (((0,), (0,)), ((), ())), preferred_element_type=F32)

    wait_for(home.at[MATE], s_recv.at[0])
    acc[...] = xs[OWN].astype(F32) + back_home(OWN)
    for pair in (A0, A1):
        wait_for(home.at[pl.ds(pair, 2)], s_recv.at[pair // 2])
        acc[...] += back_home(pair)
    wait_for(home.at[pl.ds(O0, 2)], s_recv.at[O0 // 2])
    out[...] = (acc[...] + back_home(O0)).astype(BF16)
    for ref, sem in ((xs, xs_send), (mytab, tab_send), (sums, s_send)):
        remote(ref.at[pl.ds(0, 7)], ref.at[pl.ds(0, 7)], sem, s_recv.at[0], MATE).wait_send()


def solution(mesh):
    row_spec = P(('dp', 'ep'))
    expert_spec = P('ep')
    group = mesh.shape['ep']
    assert group == 8

    def device_step(tokens, expert_ids, gate_vals, w_gate, w_up, w_down):
        rows, width = tokens.shape
        n_exp, _, hidden = w_gate.shape
        half = rows // 2
        in_hbm = functools.partial(pltpu.with_memory_space_constraint, memory_space=pltpu.HBM)
        dma = pltpu.SemaphoreType.DMA
        return pl.pallas_call(
            kernel,
            out_shape=jax.ShapeDtypeStruct((rows, width), BF16),
            in_specs=[pl.BlockSpec(memory_space=pltpu.HBM)] * 6,
            out_specs=pl.BlockSpec(memory_space=pltpu.VMEM),
            scratch_shapes=[
                pltpu.VMEM((group, rows, width), BF16),
                pltpu.VMEM((group, 2 * n_exp, half), F32),
                pltpu.VMEM((group, 2 * n_exp, half), F32),
                pltpu.VMEM((rows, rows), BF16),
                pltpu.VMEM((2, n_exp, width, hidden), BF16),
                pltpu.VMEM((n_exp, hidden, width), BF16),
                pltpu.VMEM((rows, width), BF16),
                pltpu.VMEM((group, half, width), BF16),
                pltpu.VMEM((group, half, width), BF16),
                pltpu.VMEM((rows, width), F32),
                pltpu.VMEM((group, rows), F32),
                pltpu.VMEM((expert_ids.shape[1], rows), jnp.int32),
                pltpu.VMEM((expert_ids.shape[1], rows), F32),
                dma, dma((2,)), dma((2,)), dma, dma, dma, dma((group,)), dma((2, 2)), dma((4,)), dma((4,)),
            ],
            compiler_params=pltpu.CompilerParams(collective_id=0, has_side_effects=True, vmem_limit_bytes=40 * 1024 * 1024),
        )(*map(in_hbm, (tokens, expert_ids.T, gate_vals.T, w_gate, w_up, w_down)))

    return jax.shard_map(device_step, mesh=mesh, in_specs=(row_spec, row_spec, row_spec, expert_spec, expert_spec, expert_spec),
                         out_specs=row_spec, check_vma=False)
```

time: 110 us -> 48.5 us (0.44)
  Pallas kernels: 0 us -> 47.7 us
  matrix products: 35.3 us -> 0 us
  blocking collectives: 30 us -> 0 us
  waiting for transfers between devices: 25.1 us -> 0 us
  starting transfers between devices: 10.2 us -> 0 us
  other arithmetic: 5.59 us -> 0 us
  local copies, waits for them, and re-layouts: 2.88 us -> 0.8 us
    pallas_call x0 -> x1, Pallas kernels: none -> 47.7 us  [device_step(): pl.pallas_call(kernel, out_shape=jax.ShapeDtypeStruct((rows, width), BF16...]
    dot_general x6 -> x0, matrix products: 35.3 us -> none  [the longest x1 12.5 us: expert_ffn(): jnp.einsum('lcf,lfd->lcd', hidden, w_down, preferred_element_type=jnp.flo...]
    all_to_all x1 -> x0, blocking collectives: 30 us -> none  [device_step(): lax.all_to_all(dev_sum.reshape(groups, pair_cap, d_model), 'ep', 0, 0, ti...]
    all_to_all x2 -> x0, waiting for transfers between devices: 25.1 us -> none  [the longest x1 24.4 us: device_step(): recv_rows = lax.all_to_all(send_rows, 'ep', 0, 0, tiled=True)]
    all_to_all x2 -> x0, starting transfers between devices: 10.2 us -> none  [the longest x1 6.01 us: device_step(): recv_gate = lax.all_to_all(send_gate, 'ep', 0, 0, tiled=True)]
    reduce_sum x2 -> x0, other arithmetic: 2.04 us -> none  [the longest x1 1.28 us: send_tables(): jnp.sum(jnp.where(pack_mask[:, :, :, None], gate_t[:, None, :, :], 0.0),...]
    another operation x5 -> x0, other arithmetic: 1.96 us -> none
    unnamed x8 -> x1, local copies, waits for them, and re-layouts: 1.98 us -> 0.8 us
  transfers between devices with their start and end apart: 2 -> 0, of which waited for: 2 -> 0; matrix products, arithmetic and copies ran while one was open for 5% -> 0% of each run, Pallas kernels for 0% -> 0%
where the time goes in v2:
time: 48.5 us
  Pallas kernels  47.7 us (98%)
  local copies, waits for them, and re-layouts  0.8 us (2%)
    pallas_call x1, Pallas kernels, device_step(): pl.pallas_call(kernel, out_shape=jax.ShapeDtypeStruct((rows, width), BF16...  47.7 us

profile of v2, /device:TPU:81, one launch (start us, length us, event | category | flops | bytes accessed | tf_op | source)
XLA Modules:
  0.0 48.5 jit_solution(713019034537414023)
XLA Ops:
  0.0 47.7 %shard_map.64 = bf16[256,1024]{1,0:T(8,128)(2,1)S(1)} custom-call(bf16[256,1024]{1,0:T(8,128)(2,1)} %tok.1, s32[8,256]{1,0:T(8,128)} %bitcast.2, f32[8,256]{1,0:T(8,128)} %bitcast.3, bf16[4,1024,512]{2,1,0:T(8,128)(2,1)} %wg_hbm.1, bf16[4,1024,512]{2,1,0:T(8,128)(2,1)} %wu_hbm.1, bf16[4,512,1024]{2,1,0:T(8,128)(2,1)} %wd_hbm.1), custom_call_target="tpu_custom_call" | custom-call | tf_op jit(solution)/shard_map/pallas_call | solution.py:178
  47.7 0.8 %copy.8 = bf16[256,1024]{1,0:T(8,128)(2,1)} copy(bf16[256,1024]{1,0:T(8,128)(2,1)S(1)} %shard_map.64) | data formatting | bytes 1048576

commit v3 on v2

--- a/solution.py
+++ b/solution.py
@@ -20,8 +20,8 @@
 
 
 def kernel(tok, ids_hbm, gates_hbm, wg_hbm, wu_hbm, wd_hbm, out,
-           xs, tables, mytab, tri, wgu, wd, row_in, sums, home, acc, rank_home, ids, gates,
-           tok_sem, route_sem, w_sem, xs_send, tab_send, s_send, xs_recv, half_recv, tab_recv, s_recv):
+           xs, tables, mytab, tri, wgu, wd, row_in, sums, home, acc, rank_home, ids, gates, pick, weight,
+           tok_sem, route_sem, w_sem, xs_send, tab_send, s_send, xs_recv, half_recv, tab_recv, s_recv, arrived):
     rows, half = tok.shape[0], tok.shape[0] // 2
     n_exp = wd.shape[0]
     me = lax.axis_index("ep")
@@ -43,9 +43,11 @@
     for cp in route_in:
         cp.start()
     barrier = pltpu.get_barrier_semaphore()
-    for s in range(1, 8):
+    for s in (A0, B0, MATE):
         pl.semaphore_signal(barrier, inc=1, device_id={"ep": dev[s]}, device_id_type=MESH)
-    pl.semaphore_wait(barrier, 7)
+    pl.semaphore_wait(barrier, 3)
+    for s in (A0, B0):
+        pl.semaphore_signal(arrived.at[0], inc=1, device_id={"ep": dev[s]}, device_id_type=MESH)
     tok_in.wait()
 
     part = (pl.ds(0, half), pl.ds(half, half))
@@ -55,14 +57,17 @@
         slot = seen_from(owner, to)
         remote(xs.at[owner, h], xs.at[slot, h], xs_send, recv, to).start()
 
-    for i in range(2):
+    def send_own(i):
         pass_on(OWN, part[i], A0, half_recv.at[0, i])
         pass_on(OWN, part[1 - i], B0, half_recv.at[1, i])
+
+    send_own(0)
     pass_on(OWN, whole, MATE, xs_recv.at[MATE])
     w_in = [pltpu.make_async_copy(wg_hbm, wgu.at[0], w_sem.at[0]), pltpu.make_async_copy(wu_hbm, wgu.at[1], w_sem.at[0]),
             pltpu.make_async_copy(wd_hbm, wd, w_sem.at[1])]
-    for cp in w_in:
-        cp.start()
+
+    pl.semaphore_wait(arrived.at[0], 2)
+    pl.semaphore_signal(arrived.at[1], inc=1, device_id={"ep": dev[MATE]}, device_id_type=MESH)
 
     for cp in route_in:
         cp.wait()
@@ -79,8 +84,12 @@
         mytab[s] = tab
     tri[...] = (lax.broadcasted_iota(jnp.int32, (rows, rows), 0) <=
                 lax.broadcasted_iota(jnp.int32, (rows, rows), 1)).astype(F32).astype(BF16)
+    pl.semaphore_wait(arrived.at[1], 1)
     for s in range(1, 8):
         remote(mytab.at[s], tables.at[s], tab_send, tab_recv.at[s // 2], s).start()
+    send_own(1)
+    for cp in w_in:
+        cp.start()
 
     def place(tab):
         hit = (tab != 0.0).astype(F32)
@@ -96,69 +105,76 @@
     for s in range(8):
         rank_home[s:s + 1] = place(mytab[s])
 
-    def serve(pair):
-        weight = []
+    def tables_of(pair):
+        wait_for(tables.at[pl.ds(pair[0], 2)] if pair[0] else tables.at[MATE], tab_recv.at[pair[0] // 2])
+
+    def plan(pair):
+        tables_of(pair)
+        for slot in pair:
+            tab = mytab[OWN] if slot == OWN else tables[slot]
+            hot = one_hot(rank_home[OWN:OWN + 1] if slot == OWN else place(tab))
+            pick[slot] = hot.astype(BF16)
+            g = [lax.dot_general(hot[:, j * half:(j + 1) * half], tab, (((1,), (1,)), ((), ())),
+                                 precision=lax.Precision.HIGHEST, preferred_element_type=F32) for j in range(2)]
+            weight[slot] = g[0][:, 0:n_exp] + g[1][:, n_exp:2 * n_exp]
+
+    def serve(pair, lo=0, count=half):
+        these = pl.ds(lo, count)
+        batch = row_in.at[pl.ds(0, 2 * count)]
         for i, slot in enumerate(pair):
-            tab = mytab[OWN] if slot == OWN else tables[slot]
-            pick = one_hot(rank_home[OWN:OWN + 1] if slot == OWN else place(tab))
-            row_in[part[i], :] = jnp.dot(pick.astype(BF16), xs[slot], preferred_element_type=F32).astype(BF16)
-            g = [lax.dot_general(pick[:, j * half:(j + 1) * half], tab, (((1,), (1,)), ((), ())),
-                                 precision=lax.Precision.HIGHEST, preferred_element_type=F32) for j in range(2)]
-            weight.append([g[0][:, e:e + 1] + g[1][:, n_exp + e:n_exp + e + 1] for e in range(n_exp)])
-        total = jnp.zeros(acc.shape, F32)
+            row_in[pl.ds(i * count, count), :] = jnp.dot(pick[slot, these], xs[slot], preferred_element_type=F32).astype(BF16)
+        total = jnp.zeros(batch.shape, F32)
         for e in range(n_exp):
-            a = jnp.dot(row_in[...], wgu[0, e], preferred_element_type=F32)
-            b = jnp.dot(row_in[...], wgu[1, e], preferred_element_type=F32)
+            a = jnp.dot(batch[...], wgu[0, e], preferred_element_type=F32)
+            b = jnp.dot(batch[...], wgu[1, e], preferred_element_type=F32)
             hid = (a * (1.0 / (1.0 + jnp.exp(-a))) * b).astype(BF16)
             y = jnp.dot(hid, wd[e], preferred_element_type=F32).astype(BF16).astype(F32)
-            g = jnp.concatenate([w[e] for w in weight], axis=0)
+            g = jnp.concatenate([weight[slot, these, e:e + 1] for slot in pair], axis=0)
             total = total + jnp.where(g != 0.0, g * y, 0.0)
         total = total.astype(BF16)
         for i, slot in enumerate(pair):
-            (home if slot == OWN else sums)[slot] = total[i * half:(i + 1) * half]
+            (home if slot == OWN else sums)[slot, these] = total[i * count:(i + 1) * count]
         for slot in pair:
             if slot != OWN:
-                remote(sums.at[slot], home.at[slot], s_send, s_recv.at[slot // 2], slot).start()
-
-    def tables_of(pair):
-        wait_for(tables.at[pl.ds(pair[0], 2)] if pair[0] else tables.at[MATE], tab_recv.at[pair[0] // 2])
-
-    wait_for(xs.at[MATE], xs_recv.at[MATE])
-    tables_of((OWN, MATE))
-    wait_for(wgu, w_sem.at[0])
-    w_in[2].wait()
-    serve((OWN, MATE))
+                remote(sums.at[slot, these], home.at[slot, these], s_send, s_recv.at[4 if slot == O1 else slot // 2], slot).start()
+
     for slot, on, i in ((A0, B0, 0), (B0, A0, 1)):
         wait_for(xs.at[slot, part[i]], half_recv.at[i, 0])
         pass_on(slot, part[i], on, xs_recv.at[O0])
         pass_on(slot, part[i], MATE, xs_recv.at[seen_from(slot, MATE)])
+    for pair in ((A0, B0), (A1, B1), (O0, O1), (OWN, MATE)):
+        plan(pair)
+    wait_for(wgu, w_sem.at[0])
+    w_in[2].wait()
     for slot, i in ((A0, 0), (B0, 1)):
         wait_for(xs.at[slot, part[1 - i]], half_recv.at[i, 1])
         pass_on(slot, part[1 - i], MATE, xs_recv.at[seen_from(slot, MATE)])
-    tables_of((A0, B0))
-    serve((A0, B0))
+    for lo in (0, half // 2):
+        serve((A0, B0), lo, half // 2)
     wait_for(xs.at[A1], xs_recv.at[A1])
     wait_for(xs.at[B1], xs_recv.at[B1])
-    tables_of((A1, B1))
     serve((A1, B1))
     wait_for(xs.at[O0], xs_recv.at[O0])
     pass_on(O0, whole, MATE, xs_recv.at[O1])
     wait_for(xs.at[O1], xs_recv.at[O1])
-    tables_of((O0, O1))
     serve((O0, O1))
-
-    def back_home(pair):
-        pick = jnp.concatenate([one_hot(rank_home[s:s + 1]) for s in (pair, pair + 1)], axis=0).astype(BF16)
-        got = home[pl.ds(pair, 2)].reshape(rows, home.shape[2])
-        return lax.dot_general(pick, got, (((0,), (0,)), ((), ())), preferred_element_type=F32)
+    wait_for(xs.at[MATE], xs_recv.at[MATE])
+    serve((OWN, MATE))
+
+    def back_home(*slots):
+        hot = jnp.concatenate([one_hot(rank_home[s:s + 1]) for s in slots], axis=0).astype(BF16)
+        got = home[pl.ds(slots[0], len(slots))].reshape(hot.shape[0], home.shape[2])
+        return lax.dot_general(hot, got, (((0,), (0,)), ((), ())), preferred_element_type=F32)
 
     wait_for(home.at[MATE], s_recv.at[0])
-    acc[...] = xs[OWN].astype(F32) + back_home(OWN)
+    acc[...] = xs[OWN].astype(F32) + back_home(OWN, MATE)
     for pair in (A0, A1):
         wait_for(home.at[pl.ds(pair, 2)], s_recv.at[pair // 2])
-        acc[...] += back_home(pair)
-    wait_for(home.at[pl.ds(O0, 2)], s_recv.at[O0 // 2])
-    out[...] = (acc[...] + back_home(O0)).astype(BF16)
+        acc[...] += back_home(pair, pair + 1)
+    wait_for(home.at[O0], s_recv.at[O0 // 2])
+    acc[...] += back_home(O0)
+    wait_for(home.at[O1], s_recv.at[4])
+    out[...] = (acc[...] + back_home(O1)).astype(BF16)
     for ref, sem in ((xs, xs_send), (mytab, tab_send), (sums, s_send)):
         remote(ref.at[pl.ds(0, 7)], ref.at[pl.ds(0, 7)], sem, s_recv.at[0], MATE).wait_send()
 
@@ -194,7 +210,10 @@
                 pltpu.VMEM((group, rows), F32),
                 pltpu.VMEM((expert_ids.shape[1], rows), jnp.int32),
                 pltpu.VMEM((expert_ids.shape[1], rows), F32),
-                dma, dma((2,)), dma((2,)), dma, dma, dma, dma((group,)), dma((2, 2)), dma((4,)), dma((4,)),
+                pltpu.VMEM((group, half, rows), BF16),
+                pltpu.VMEM((group, half, n_exp), F32),
+                dma, dma((2,)), dma((2,)), dma, dma, dma, dma((group,)), dma((2, 2)), dma((4,)), dma((5,)),
+                pltpu.SemaphoreType.REGULAR((2,)),
             ],
             compiler_params=pltpu.CompilerParams(collective_id=0, has_side_effects=True, vmem_limit_bytes=40 * 1024 * 1024),
         )(*map(in_hbm, (tokens, expert_ids.T, gate_vals.T, w_gate, w_up, w_down)))

time: 48.5 us -> 46.7 us (0.963)
  Pallas kernels: 47.7 us -> 45.4 us
    pallas_call x1, Pallas kernels: 47.7 us -> 45.4 us  [device_step(): pl.pallas_call(kernel, out_shape=jax.ShapeDtypeStruct((rows, width), BF16...]
where the time goes in v3:
time: 46.7 us; the launch traced here: 46.2 us
  Pallas kernels  45.4 us (97%)
  local copies, waits for them, and re-layouts  0.8 us (2%)
    pallas_call x1, Pallas kernels, device_step(): pl.pallas_call(kernel, out_shape=jax.ShapeDtypeStruct((rows, width), BF16...  45.4 us

profile of v3, /device:TPU:81, one launch (start us, length us, event | category | flops | bytes accessed | tf_op | source)
XLA Modules:
  0.0 46.2 jit_solution(1289732389717842200)
XLA Ops:
  0.0 45.4 %shard_map.64 = bf16[256,1024]{1,0:T(8,128)(2,1)S(1)} custom-call(bf16[256,1024]{1,0:T(8,128)(2,1)} %tok.1, s32[8,256]{1,0:T(8,128)} %bitcast.2, f32[8,256]{1,0:T(8,128)} %bitcast.3, bf16[4,1024,512]{2,1,0:T(8,128)(2,1)} %wg_hbm.1, bf16[4,1024,512]{2,1,0:T(8,128)(2,1)} %wu_hbm.1, bf16[4,512,1024]{2,1,0:T(8,128)(2,1)} %wd_hbm.1), custom_call_target="tpu_custom_call" | custom-call | tf_op jit(solution)/shard_map/pallas_call | solution.py:194
  45.4 0.8 %copy.8 = bf16[256,1024]{1,0:T(8,128)(2,1)} copy(bf16[256,1024]{1,0:T(8,128)(2,1)S(1)} %shard_map.64) | data formatting | bytes 1048576

commit v4 on v3

--- a/solution.py
+++ b/solution.py
@@ -20,8 +20,9 @@
 
 
 def kernel(tok, ids_hbm, gates_hbm, wg_hbm, wu_hbm, wd_hbm, out,
-           xs, tables, mytab, tri, wgu, wd, row_in, sums, home, acc, rank_home, ids, gates, pick, weight,
-           tok_sem, route_sem, w_sem, xs_send, tab_send, s_send, xs_recv, half_recv, tab_recv, s_recv, arrived):
+           xs, tables, mytab, tri, wgu, wd, row_in, sums, home, acc, rank_home, ids, gates, pick, weight, home_near, pick_near,
+           tok_sem, route_sem, w_sem, xs_send, tab_send, s_send, xs_recv, half_recv, tab_recv, s_recv, arrived,
+           relay, relay_send, relay_recv):
     rows, half = tok.shape[0], tok.shape[0] // 2
     n_exp = wd.shape[0]
     me = lax.axis_index("ep")
@@ -37,14 +38,14 @@
     def wait_for(ref, sem):
         remote(ref, ref, xs_send, sem, MATE).wait_recv()
 
+    barrier = pltpu.get_barrier_semaphore()
+    for s in (A0, B0, MATE):
+        pl.semaphore_signal(barrier, inc=1, device_id={"ep": dev[s]}, device_id_type=MESH)
     tok_in = pltpu.make_async_copy(tok, xs.at[OWN], tok_sem)
     tok_in.start()
     route_in = [pltpu.make_async_copy(h, v, route_sem.at[i]) for i, (h, v) in enumerate(((ids_hbm, ids), (gates_hbm, gates)))]
     for cp in route_in:
         cp.start()
-    barrier = pltpu.get_barrier_semaphore()
-    for s in (A0, B0, MATE):
-        pl.semaphore_signal(barrier, inc=1, device_id={"ep": dev[s]}, device_id_type=MESH)
     pl.semaphore_wait(barrier, 3)
     for s in (A0, B0):
         pl.semaphore_signal(arrived.at[0], inc=1, device_id={"ep": dev[s]}, device_id_type=MESH)
@@ -118,9 +119,21 @@
                                  precision=lax.Precision.HIGHEST, preferred_element_type=F32) for j in range(2)]
             weight[slot] = g[0][:, 0:n_exp] + g[1][:, n_exp:2 * n_exp]
 
+    quarter = (pl.ds(0, half // 2), pl.ds(half // 2, half // 2))
+
+    def first_hop(slot):
+        for i, by in enumerate((A0, B0)):
+            remote(sums.at[slot, quarter[i]], relay.at[i, slot - O0], s_send, relay_recv.at[i, slot - O0], by).start()
+
+    def second_hop(slot):
+        for i, to in enumerate((B0, A0)):
+            wait_for(relay.at[i, slot - O0], relay_recv.at[i, slot - O0])
+            remote(relay.at[i, slot - O0], home.at[slot, quarter[i]], relay_send, s_recv.at[O0 // 2],
+                   to if slot == O0 else seen_from(to, MATE)).start()
+
     def serve(pair, lo=0, count=half):
         these = pl.ds(lo, count)
-        batch = row_in.at[pl.ds(0, 2 * count)]
+        batch = row_in.at[pl.ds(0, len(pair) * count)]
         for i, slot in enumerate(pair):
             row_in[pl.ds(i * count, count), :] = jnp.dot(pick[slot, these], xs[slot], preferred_element_type=F32).astype(BF16)
         total = jnp.zeros(batch.shape, F32)
@@ -133,10 +146,7 @@
             total = total + jnp.where(g != 0.0, g * y, 0.0)
         total = total.astype(BF16)
         for i, slot in enumerate(pair):
-            (home if slot == OWN else sums)[slot, these] = total[i * count:(i + 1) * count]
-        for slot in pair:
-            if slot != OWN:
-                remote(sums.at[slot, these], home.at[slot, these], s_send, s_recv.at[4 if slot == O1 else slot // 2], slot).start()
+            (home if slot is OWN else sums)[slot, these] = total[i * count:(i + 1) * count]
 
     for slot, on, i in ((A0, B0, 0), (B0, A0, 1)):
         wait_for(xs.at[slot, part[i]], half_recv.at[i, 0])
@@ -149,17 +159,40 @@
     for slot, i in ((A0, 0), (B0, 1)):
         wait_for(xs.at[slot, part[1 - i]], half_recv.at[i, 1])
         pass_on(slot, part[1 - i], MATE, xs_recv.at[seen_from(slot, MATE)])
-    for lo in (0, half // 2):
-        serve((A0, B0), lo, half // 2)
+    ones = [A0 + 2 * (1 - c), B0 + 2 * (1 - c)]
+    zeros = [A0 + 2 * c, B0 + 2 * c]
+
+    def serve_neighbours(pair, core, i):
+        serve(pair, i * half // 2, half // 2)
+
+    def answer_neighbours(pair, core, i):
+        for slot, chip in zip(pair, (CHIP[A0], CHIP[B0])):
+            pltpu.make_async_remote_copy(src_ref=sums.at[slot, quarter[i]], dst_ref=home_near.at[i, slot - A0],
+                                         send_sem=s_send, recv_sem=s_recv.at[1 + i],
+                                         device_id={"ep": 2 * x_of[chip] + core}, device_id_type=MESH).start()
+
+    first, early, late, last = ([A0, B0], c, 0), (ones, 1, 1), ([A1, B1], 1 - c, 0), (zeros, 0, 1)
+    serve_neighbours(*first)
+    answer_neighbours(*first)
     wait_for(xs.at[A1], xs_recv.at[A1])
     wait_for(xs.at[B1], xs_recv.at[B1])
-    serve((A1, B1))
+    serve_neighbours(*early)
+    answer_neighbours(*early)
     wait_for(xs.at[O0], xs_recv.at[O0])
     pass_on(O0, whole, MATE, xs_recv.at[O1])
+    serve([O0])
+    first_hop(O0)
     wait_for(xs.at[O1], xs_recv.at[O1])
-    serve((O0, O1))
+    serve([O1])
+    first_hop(O1)
+    for rest, slot in ((late, O0), (last, O1)):
+        serve_neighbours(*rest)
+        second_hop(slot)
+    answer_neighbours(*late)
+    answer_neighbours(*last)
     wait_for(xs.at[MATE], xs_recv.at[MATE])
-    serve((OWN, MATE))
+    serve([OWN, MATE])
+    remote(sums.at[MATE], home.at[MATE], s_send, s_recv.at[0], MATE).start()
 
     def back_home(*slots):
         hot = jnp.concatenate([one_hot(rank_home[s:s + 1]) for s in slots], axis=0).astype(BF16)
@@ -168,15 +201,25 @@
 
     wait_for(home.at[MATE], s_recv.at[0])
     acc[...] = xs[OWN].astype(F32) + back_home(OWN, MATE)
-    for pair in (A0, A1):
-        wait_for(home.at[pl.ds(pair, 2)], s_recv.at[pair // 2])
-        acc[...] += back_home(pair, pair + 1)
-    wait_for(home.at[O0], s_recv.at[O0 // 2])
-    acc[...] += back_home(O0)
-    wait_for(home.at[O1], s_recv.at[4])
-    out[...] = (acc[...] + back_home(O1)).astype(BF16)
+    square = (rows, rows)
+    eye = (lax.broadcasted_iota(jnp.int32, square, 0) == lax.broadcasted_iota(jnp.int32, square, 1)).astype(F32).astype(BF16)
+    near = [one_hot(rank_home[s:s + 1]) for s in (A0, B0, A1, B1)]
+    for i in range(2):
+        hot = jnp.concatenate([h[i * half // 2:(i + 1) * half // 2] for h in near], axis=0).astype(BF16)
+        pick_near[i] = lax.dot_general(hot, eye, (((0,), (0,)), ((), ())), preferred_element_type=F32).astype(BF16)
+
+    def near_sum(i):
+        return jnp.dot(pick_near[i], home_near[i].reshape(rows, home.shape[2]), preferred_element_type=F32)
+
+    wait_for(home.at[pl.ds(O0, 2)], s_recv.at[3])
+    acc[...] += back_home(O0, O1)
+    wait_for(home_near.at[0], s_recv.at[1])
+    acc[...] += near_sum(0)
     for ref, sem in ((xs, xs_send), (mytab, tab_send), (sums, s_send)):
         remote(ref.at[pl.ds(0, 7)], ref.at[pl.ds(0, 7)], sem, s_recv.at[0], MATE).wait_send()
+    remote(relay, relay, relay_send, s_recv.at[0], MATE).wait_send()
+    wait_for(home_near.at[1], s_recv.at[2])
+    out[...] = (acc[...] + near_sum(1)).astype(BF16)
 
 
 def solution(mesh):
@@ -212,8 +255,12 @@
                 pltpu.VMEM((expert_ids.shape[1], rows), F32),
                 pltpu.VMEM((group, half, rows), BF16),
                 pltpu.VMEM((group, half, n_exp), F32),
-                dma, dma((2,)), dma((2,)), dma, dma, dma, dma((group,)), dma((2, 2)), dma((4,)), dma((5,)),
+                pltpu.VMEM((2, 4, half // 2, width), BF16),
+                pltpu.VMEM((2, rows, rows), BF16),
+                dma, dma((2,)), dma((2,)), dma, dma, dma, dma((group,)), dma((2, 2)), dma((4,)), dma((4,)),
                 pltpu.SemaphoreType.REGULAR((2,)),
+                pltpu.VMEM((2, 2, half // 2, width), BF16),
+                dma, dma((2, 2)),
             ],
             compiler_params=pltpu.CompilerParams(collective_id=0, has_side_effects=True, vmem_limit_bytes=40 * 1024 * 1024),
         )(*map(in_hbm, (tokens, expert_ids.T, gate_vals.T, w_gate, w_up, w_down)))

time: 46.7 us -> 46.2 us (0.989)
  no operation moved by 1% of the time
where the time goes in v4:
time: 46.2 us; the launch traced here: 45.9 us
  Pallas kernels  45.1 us (98%)
  local copies, waits for them, and re-layouts  0.8 us (2%)
    pallas_call x1, Pallas kernels, device_step(): pl.pallas_call(kernel, out_shape=jax.ShapeDtypeStruct((rows, width), BF16...  45.1 us

profile of v4, /device:TPU:81, one launch (start us, length us, event | category | flops | bytes accessed | tf_op | source)
XLA Modules:
  0.0 45.9 jit_solution(389007273503874993)
XLA Ops:
  0.0 45.1 %shard_map.64 = bf16[256,1024]{1,0:T(8,128)(2,1)S(1)} custom-call(bf16[256,1024]{1,0:T(8,128)(2,1)} %tok.1, s32[8,256]{1,0:T(8,128)} %bitcast.2, f32[8,256]{1,0:T(8,128)} %bitcast.3, bf16[4,1024,512]{2,1,0:T(8,128)(2,1)} %wg_hbm.1, bf16[4,1024,512]{2,1,0:T(8,128)(2,1)} %wu_hbm.1, bf16[4,512,1024]{2,1,0:T(8,128)(2,1)} %wd_hbm.1), custom_call_target="tpu_custom_call" | custom-call | tf_op jit(solution)/shard_map/pallas_call | solution.py:237
  45.1 0.8 %copy.8 = bf16[256,1024]{1,0:T(8,128)(2,1)} copy(bf16[256,1024]{1,0:T(8,128)(2,1)S(1)} %shard_map.64) | data formatting | bytes 1048576

commit v5 on v4

--- a/solution.py
+++ b/solution.py
@@ -54,6 +54,9 @@
     part = (pl.ds(0, half), pl.ds(half, half))
     whole = pl.ds(0, rows)
 
+    def block_sem(slot):
+        return xs_recv.at[{MATE: 0, A1: 1, B1: 1, O0: 2, O1: 3}[slot]]
+
     def pass_on(owner, h, to, recv):
         slot = seen_from(owner, to)
         remote(xs.at[owner, h], xs.at[slot, h], xs_send, recv, to).start()
@@ -63,7 +66,7 @@
         pass_on(OWN, part[1 - i], B0, half_recv.at[1, i])
 
     send_own(0)
-    pass_on(OWN, whole, MATE, xs_recv.at[MATE])
+    pass_on(OWN, whole, MATE, block_sem(MATE))
     w_in = [pltpu.make_async_copy(wg_hbm, wgu.at[0], w_sem.at[0]), pltpu.make_async_copy(wu_hbm, wgu.at[1], w_sem.at[0]),
             pltpu.make_async_copy(wd_hbm, wd, w_sem.at[1])]
 
@@ -87,7 +90,7 @@
                 lax.broadcasted_iota(jnp.int32, (rows, rows), 1)).astype(F32).astype(BF16)
     pl.semaphore_wait(arrived.at[1], 1)
     for s in range(1, 8):
-        remote(mytab.at[s], tables.at[s], tab_send, tab_recv.at[s // 2], s).start()
+        remote(mytab.at[s], tables.at[s], tab_send, tab_recv, s).start()
     send_own(1)
     for cp in w_in:
         cp.start()
@@ -106,11 +109,7 @@
     for s in range(8):
         rank_home[s:s + 1] = place(mytab[s])
 
-    def tables_of(pair):
-        wait_for(tables.at[pl.ds(pair[0], 2)] if pair[0] else tables.at[MATE], tab_recv.at[pair[0] // 2])
-
     def plan(pair):
-        tables_of(pair)
         for slot in pair:
             tab = mytab[OWN] if slot == OWN else tables[slot]
             hot = one_hot(rank_home[OWN:OWN + 1] if slot == OWN else place(tab))
@@ -123,12 +122,12 @@
 
     def first_hop(slot):
         for i, by in enumerate((A0, B0)):
-            remote(sums.at[slot, quarter[i]], relay.at[i, slot - O0], s_send, relay_recv.at[i, slot - O0], by).start()
+            remote(sums.at[slot, quarter[i]], relay.at[slot - O0, i], s_send, relay_recv.at[slot - O0, i], by).start()
 
     def second_hop(slot):
         for i, to in enumerate((B0, A0)):
-            wait_for(relay.at[i, slot - O0], relay_recv.at[i, slot - O0])
-            remote(relay.at[i, slot - O0], home.at[slot, quarter[i]], relay_send, s_recv.at[O0 // 2],
+            wait_for(relay.at[slot - O0, i], relay_recv.at[slot - O0, i])
+            remote(relay.at[slot - O0, i], home.at[slot, quarter[i]], relay_send, s_recv.at[O0 // 2],
                    to if slot == O0 else seen_from(to, MATE)).start()
 
     def serve(pair, lo=0, count=half):
@@ -150,15 +149,16 @@
 
     for slot, on, i in ((A0, B0, 0), (B0, A0, 1)):
         wait_for(xs.at[slot, part[i]], half_recv.at[i, 0])
-        pass_on(slot, part[i], on, xs_recv.at[O0])
-        pass_on(slot, part[i], MATE, xs_recv.at[seen_from(slot, MATE)])
+        pass_on(slot, part[i], on, block_sem(O0))
+        pass_on(slot, part[i], MATE, block_sem(seen_from(slot, MATE)))
+    wait_for(tables.at[pl.ds(1, 7)], tab_recv)
     for pair in ((A0, B0), (A1, B1), (O0, O1), (OWN, MATE)):
         plan(pair)
     wait_for(wgu, w_sem.at[0])
     w_in[2].wait()
     for slot, i in ((A0, 0), (B0, 1)):
         wait_for(xs.at[slot, part[1 - i]], half_recv.at[i, 1])
-        pass_on(slot, part[1 - i], MATE, xs_recv.at[seen_from(slot, MATE)])
+        pass_on(slot, part[1 - i], MATE, block_sem(seen_from(slot, MATE)))
     ones = [A0 + 2 * (1 - c), B0 + 2 * (1 - c)]
     zeros = [A0 + 2 * c, B0 + 2 * c]
 
@@ -174,15 +174,14 @@
     first, early, late, last = ([A0, B0], c, 0), (ones, 1, 1), ([A1, B1], 1 - c, 0), (zeros, 0, 1)
     serve_neighbours(*first)
     answer_neighbours(*first)
-    wait_for(xs.at[A1], xs_recv.at[A1])
-    wait_for(xs.at[B1], xs_recv.at[B1])
+    wait_for(xs.at[pl.ds(A1, 2)], block_sem(A1))
     serve_neighbours(*early)
     answer_neighbours(*early)
-    wait_for(xs.at[O0], xs_recv.at[O0])
-    pass_on(O0, whole, MATE, xs_recv.at[O1])
+    wait_for(xs.at[O0], block_sem(O0))
+    pass_on(O0, whole, MATE, block_sem(O1))
     serve([O0])
     first_hop(O0)
-    wait_for(xs.at[O1], xs_recv.at[O1])
+    wait_for(xs.at[O1], block_sem(O1))
     serve([O1])
     first_hop(O1)
     for rest, slot in ((late, O0), (last, O1)):
@@ -190,7 +189,7 @@
         second_hop(slot)
     answer_neighbours(*late)
     answer_neighbours(*last)
-    wait_for(xs.at[MATE], xs_recv.at[MATE])
+    wait_for(xs.at[MATE], block_sem(MATE))
     serve([OWN, MATE])
     remote(sums.at[MATE], home.at[MATE], s_send, s_recv.at[0], MATE).start()
 
@@ -257,7 +256,7 @@
                 pltpu.VMEM((group, half, n_exp), F32),
                 pltpu.VMEM((2, 4, half // 2, width), BF16),
                 pltpu.VMEM((2, rows, rows), BF16),
-                dma, dma((2,)), dma((2,)), dma, dma, dma, dma((group,)), dma((2, 2)), dma((4,)), dma((4,)),
+                dma, dma((2,)), dma((2,)), dma, dma, dma, dma((4,)), dma((2, 2)), dma, dma((4,)),
                 pltpu.SemaphoreType.REGULAR((2,)),
                 pltpu.VMEM((2, 2, half // 2, width), BF16),
                 dma, dma((2, 2)),

time: 46.2 us -> 46.1 us (level)
  no operation moved by 1% of the time
where the time goes in v5:
time: 46.1 us; the launch traced here: 45.9 us
  Pallas kernels  45.1 us (98%)
  local copies, waits for them, and re-layouts  0.8 us (2%)
    pallas_call x1, Pallas kernels, device_step(): pl.pallas_call(kernel, out_shape=jax.ShapeDtypeStruct((rows, width), BF16...  45.1 us

profile of v5, /device:TPU:81, one launch (start us, length us, event | category | flops | bytes accessed | tf_op | source)
XLA Modules:
  0.0 45.9 jit_solution(10148800577114407504)
XLA Ops:
  0.0 45.1 %shard_map.64 = bf16[256,1024]{1,0:T(8,128)(2,1)S(1)} custom-call(bf16[256,1024]{1,0:T(8,128)(2,1)} %tok.1, s32[8,256]{1,0:T(8,128)} %bitcast.2, f32[8,256]{1,0:T(8,128)} %bitcast.3, bf16[4,1024,512]{2,1,0:T(8,128)(2,1)} %wg_hbm.1, bf16[4,1024,512]{2,1,0:T(8,128)(2,1)} %wu_hbm.1, bf16[4,512,1024]{2,1,0:T(8,128)(2,1)} %wd_hbm.1), custom_call_target="tpu_custom_call" | custom-call | tf_op jit(solution)/shard_map/pallas_call | solution.py:236
  45.1 0.8 %copy.8 = bf16[256,1024]{1,0:T(8,128)(2,1)} copy(bf16[256,1024]{1,0:T(8,128)(2,1)S(1)} %shard_map.64) | data formatting | bytes 1048576
